TPU v7x, 32 devices: a whole 2x2x4 slice. The times are simulated.
32 devices in a mesh: task: 8 (over z, core), tp: 4 (over y, x).
Axes of the slice: x: 2, y: 2, z: 4, core: 2. Of those that a mesh axis runs over, the one named last changes fastest.
Arguments:
- support_x: bfloat16 [8, 384, 3584], P('task'), may hold values from -6 to 6
- adapter_a: bfloat16 [8, 3584, 64], P('task'), may hold values from -0.09375 to 0.09375
- gate_pre: bfloat16 [8, 384, 10240], P('task', None, 'tp'), may hold values from -6 to 6
- lengths: int32 [8], P('task'), may hold values from 128 to 384, as said below
- damping: float32 [8], P('task'), may hold values from 0.03 to 0.3
- down_w: bfloat16 [10240, 3584], P('tp', 'task'), may hold values from -0.0625 to 0.0625
- grad_b: float32 [8, 64, 10240], P('task', None, 'tp'), may hold values from -6 to 6
Outputs:
- solution: float32 [8, 64, 10240], P('task', None, 'tp')
- residual: float32 [8, 64, 10240], P('task', None, 'tp')
Inputs may be any that keep to these rules, and one draw needn't show every extreme that they name: `lengths`: each a multiple of 128; some task has exactly 384.
All inputs are finite; a program needn't handle non-finite values.
Results may differ from a plain program's by a relative error of at most 0.033.
Values may be sent and summed in bfloat16 or wider, within the bound.
A program may use at most 64 MiB of HBM per device.

v0:
```python
import jax
import jax.numpy as jnp
from jax import lax
from jax.sharding import PartitionSpec as P

ITERS = 2


def shards(support_x, adapter_a, gate_pre, lengths, damping, down_w, grad_b):
    down_full = lax.all_gather(down_w, "task", axis=1, tiled=True)
    features = jnp.dot(support_x[0], adapter_a[0], preferred_element_type=jnp.float32).astype(
        jnp.bfloat16
    )
    positions = lax.broadcasted_iota(jnp.int32, (gate_pre.shape[1], 1), 0)
    gated = jnp.where(
        positions < lengths[0], jax.nn.silu(gate_pre[0].astype(jnp.float32)), 0.0
    ).astype(jnp.bfloat16)
    tokens_live = lengths[0].astype(jnp.float32)
    damping_rate = damping[0]

    def transposed(mixed_rows):
        return lax.dot_general(
            mixed_rows, down_full, (((1,), (1,)), ((), ())), preferred_element_type=jnp.float32
        )

    def apply(vector):
        inner = jnp.dot(features, vector.astype(jnp.bfloat16), preferred_element_type=jnp.float32)
        active = (gated * inner).astype(jnp.bfloat16)
        partial_sum = jnp.dot(active, down_full, preferred_element_type=jnp.float32)
        mixed = lax.psum(partial_sum.astype(jnp.bfloat16), "tp")
        second = (gated * transposed(mixed)).astype(jnp.bfloat16)
        product = lax.dot_general(
            features, second, (((0,), (0,)), ((), ())), preferred_element_type=jnp.float32
        )
        return product / tokens_live + damping_rate * vector

    def paired_sums(vector, image):
        return lax.psum((jnp.sum(vector * vector), jnp.sum(vector * image)), "tp")

    target = grad_b[0]
    solution = jnp.zeros_like(target)
    residual = target
    image = apply(residual)
    norm_now, product = paired_sums(residual, image)
    alpha = norm_now / product
    direction, along = (residual, image)
    for step in range(ITERS):
        solution = solution + alpha * direction
        residual = residual - alpha * along
        if step + 1 < ITERS:
            image = apply(residual)
            norm_next, product = paired_sums(residual, image)
            ratio = norm_next / norm_now
            alpha = norm_next / (product - ratio * norm_next / alpha)
            direction = residual + ratio * direction
            along = image + ratio * along
            norm_now = norm_next
    return (solution[None], residual[None])


def solution(mesh):
    in_specs = (
        P("task", None, None),
        P("task", None, None),
        P("task", None, "tp"),
        P("task"),
        P("task"),
        P("tp", "task"),
        P("task", None, "tp"),
    )
    out_specs = (P("task", None, "tp"), P("task", None, "tp"))
    return jax.shard_map(shards, mesh=mesh, in_specs=in_specs, out_specs=out_specs, check_vma=False)
```

profile of v0, /device:TPU:0, one launch (start us, length us, event | category | flops | bytes accessed | tf_op | source)
XLA Modules:
  0.0 429.8 jit_solution(7831728093009791851)
XLA Ops:
  7.2 0.0 copy-start
  7.2 0.0 copy-start.1
  7.2 0.0 all-gather.2.cloned.1.call-start
  7.2 0.7 all-gather.2.cloned.1.call-update
  7.9 0.0 all-reduce.5.cloned.1.call-start
  8.9 0.1 copy-done
  8.9 2.0 fusion.13
  10.9 165.4 %all-gather.2.cloned.1.call-done = bf16[2560,3584]{0,1:T(8,128)(2,1)} async-done(((bf16[2560,448]{0,1:T(8,128)(2,1)}), bf16[2560,3584]{0,1:T(8,128)(2,1)}) %all-gather.2.cloned.1.call-update) | async-done | bytes 18350096 | tf_op jit(solution)/shard_map/all_gather | solution.py:10
  176.4 0.0 copy-done.1
  176.4 14.4 %convolution_convert_fusion.1 = bf16[384,3584]{1,0:T(8,128)(2,1)} fusion(bf16[2560,3584]{0,1:T(8,128)(2,1)} %all-gather.2.cloned.1.call-done, bf16[384,64]{0,1:T(8,128)(2,1)S(1)} %fusion.13, f32[1,64,2560]{2,1,0:T(8,128)S(1)} %copy-done.1, bf16[1,384,2560]{2,1,0:T(8,128)(2,1)} %param.9, pred[384]{0:T(512)(128)(4,1)S(1)} %iota_compare_fusion), kind=kOutput, calls=%fused_computation.5 | convolution fusion | flops 7183466496 | bytes 23773568 | tf_op jit(solution)/shard_map/dot_general | solution.py:29
  190.8 0.0 all-reduce.5.cloned.1.call-update
  190.8 0.0 all-reduce.7.cloned.1.call-start
  191.5 78.1 %all-reduce.5.cloned.1.call-done = bf16[384,3584]{1,0:T(8,128)(2,1)} async-done(((bf16[384,3584]{1,0:T(8,128)(2,1)}), bf16[384,3584]{1,0:T(8,128)(2,1)}) %all-reduce.5.cloned.1.call-update) | async-done | bytes 2752528 | tf_op jit(solution)/shard_map/psum | solution.py:30
  269.5 14.3 %fusion.17 = (f32[]{:T(128)}, f32[]{:T(128)}, f32[64,2560]{1,0:T(8,128)}) fusion(f32[1,64,2560]{2,1,0:T(8,128)S(1)} %copy-done.1, f32[]{:T(128)} %bitcast.71, f32[]{:T(128)S(6)} %convert_element_type.54, bf16[384,64]{0,1:T(8,128)(2,1)S(1)} %fusion.13, bf16[384,3584]{1,0:T(8,128)(2,1)} %all-reduce.5.cloned.1.call-done, ...), kind=kOutput, calls=%fused_computation.32 | convolution fusion | flops 7183237120 | bytes 24428944 | tf_op jit(solution)/shard_map/dot_general | solution.py:32
  283.9 9.7 %all-reduce.1 = (f32[]{:T(128)}, f32[]{:T(128)}) all-reduce(f32[]{:T(128)} %get-tuple-element.5, f32[]{:T(128)} %get-tuple-element.4), channel_id=1, replica_groups=mesh['task'=8,'tp'=4] {'tp'}, use_global_device_ids=true, to_apply=%region_1.2 | all-reduce | flops 2 | bytes 16 | tf_op jit(solution)/shard_map/psum | solution.py:38
  294.9 2.0 bitcast_subtract_fusion
  296.9 14.6 %convolution_convert_fusion = bf16[384,3584]{1,0:T(8,128)(2,1)} fusion(bf16[2560,3584]{0,1:T(8,128)(2,1)} %all-gather.2.cloned.1.call-done, bf16[384,64]{0,1:T(8,128)(2,1)S(1)} %fusion.13, f32[64,2560]{1,0:T(8,128)} %bitcast_subtract_fusion, bf16[1,384,2560]{2,1,0:T(8,128)(2,1)} %param.9, pred[384]{0:T(512)(128)(4,1)S(1)} %iota_compare_fusion), kind=kOutput, calls=%fused_computation.4 | convolution fusion | flops 7183630336 | bytes 23773568 | tf_op jit(solution)/shard_map/dot_general | solution.py:29
  311.5 0.0 all-reduce.7.cloned.1.call-update
  311.5 80.5 %all-reduce.7.cloned.1.call-done = bf16[384,3584]{1,0:T(8,128)(2,1)} async-done(((bf16[384,3584]{1,0:T(8,128)(2,1)}), bf16[384,3584]{1,0:T(8,128)(2,1)}) %all-reduce.7.cloned.1.call-update) | async-done | bytes 2752528 | tf_op jit(solution)/shard_map/psum | solution.py:30
  392.1 14.7 %multiply_reduce_fusion = (f32[]{:T(128)}, f32[]{:T(128)}, f32[64,2560]{1,0:T(8,128)}) fusion(f32[64,2560]{1,0:T(8,128)} %bitcast_subtract_fusion, f32[]{:T(128)} %bitcast.72, f32[]{:T(128)S(6)} %convert_element_type.54, bf16[384,64]{0,1:T(8,128)(2,1)S(1)} %fusion.13, bf16[384,3584]{1,0:T(8,128)(2,1)} %all-reduce.7.cloned.1.call-done, ...), kind=kOutput, calls=%fused_computation.38 | convolution fusion | flops 7183237120 | bytes 24428944 | tf_op jit(solution)/shard_map/dot_general | solution.py:32
  406.8 9.5 %all-reduce = (f32[]{:T(128)}, f32[]{:T(128)}) all-reduce(f32[]{:T(128)} %get-tuple-element.3, f32[]{:T(128)} %get-tuple-element.2), channel_id=1, replica_groups=mesh['task'=8,'tp'=4] {'tp'}, use_global_device_ids=true, to_apply=%region_6.7 | all-reduce | flops 2 | bytes 16 | tf_op jit(solution)/shard_map/psum | solution.py:38
  420.5 2.7 subtract_bitcast_fusion
  (1 shorter events, 0.0 us)
Async XLA Ops:
  7.2 1.8 copy-start
  7.2 169.2 %copy-start.1 = (f32[1,64,2560]{2,1,0:T(8,128)S(1)}, f32[1,64,2560]{2,1,0:T(8,128)}, u32[]{:S(2)}) copy-start(f32[1,64,2560]{2,1,0:T(8,128)} %param.13) | copy-start | bytes 1966084
  7.2 169.2 %all-gather.2.cloned.1.call-start = ((), (), s32[]{:S(2)}) async-start(), calls=%async_computation | async-start | bytes 20643840 | tf_op jit(solution)/shard_map/all_gather | solution.py:10
  7.9 261.6 %all-reduce.5.cloned.1.call-start = ((), (), s32[]{:S(2)}) async-start(), calls=%async_computation.1 | async-start | bytes 5505024 | tf_op jit(solution)/shard_map/psum | solution.py:30
  190.8 201.3 %all-reduce.7.cloned.1.call-start = ((), (), s32[]{:S(2)}) async-start(), calls=%async_computation.2 | async-start | bytes 5505024 | tf_op jit(solution)/shard_map/psum | solution.py:30
Sparse Core Ops, SparseCore 0:
  9.6 166.6 all-gather.1
  190.9 78.5 all-reduce.4
  311.6 80.3 all-reduce.6
where the time goes:
time: 430 us
  waiting for transfers between devices  325 us (76%)
  matrix products  60 us (14%)
  between operations  20.8 us (5%)
  blocking collectives  19.3 us (4%)
  other arithmetic  4.75 us (1%)
    all_gather x1, waiting for transfers between devices, shards(): down_full = lax.all_gather(down_w, 'task', axis=1, tiled=True)  165 us
    psum x2, waiting for transfers between devices, apply(): mixed = lax.psum(partial_sum.astype(jnp.bfloat16), 'tp')  159 us
    dot_general x2, matrix products, apply(): lax.dot_general(features, second, (((0,), (0,)), ((), ())), preferred_ele...  29 us
    dot_general x2, matrix products, apply(): partial_sum = jnp.dot(active, down_full, preferred_element_type=jnp.float32)  29 us
    psum x2, blocking collectives, paired_sums(): return lax.psum((jnp.sum(vector * vector), jnp.sum(vector * image)), 'tp')  19.3 us
  transfers between devices with their start and end apart: 3, of which 3 were waited for; matrix products, arithmetic and copies ran while one was open for 0% of the time, Pallas kernels for 0%

commit v1 on v0

--- a/solution.py
+++ b/solution.py
@@ -27,7 +27,7 @@
         inner = jnp.dot(features, vector.astype(jnp.bfloat16), preferred_element_type=jnp.float32)
         active = (gated * inner).astype(jnp.bfloat16)
         partial_sum = jnp.dot(active, down_full, preferred_element_type=jnp.float32)
-        mixed = lax.psum(partial_sum.astype(jnp.bfloat16), "tp")
+        mixed = jnp.sum(lax.all_gather(partial_sum.astype(jnp.bfloat16), "tp"), axis=0)
         second = (gated * transposed(mixed)).astype(jnp.bfloat16)
         product = lax.dot_general(
             features, second, (((0,), (0,)), ((), ())), preferred_element_type=jnp.float32

time: 430 us -> 505 us (1.17)
  waiting for transfers between devices: 325 us -> 383 us
  other arithmetic: 4.75 us -> 21.1 us
    all_gather x0 -> x2, waiting for transfers between devices: none -> 216 us  [apply(): lax.all_gather(partial_sum.astype(jnp.bfloat16), 'tp')]
    psum x2 -> x0, waiting for transfers between devices: 159 us -> none  [apply(): mixed = lax.psum(partial_sum.astype(jnp.bfloat16), 'tp')]
    reduce_sum x0 -> x2, other arithmetic: none -> 16.3 us  [apply(): jnp.sum(lax.all_gather(partial_sum.astype(jnp.bfloat16), 'tp'), axis=0)]
where the time goes in v1:
time: 505 us
  waiting for transfers between devices  383 us (76%)
  matrix products  60.5 us (12%)
  other arithmetic  21.1 us (4%)
  between operations  21.1 us (4%)
  blocking collectives  19.4 us (4%)
    all_gather x2, waiting for transfers between devices, apply(): lax.all_gather(partial_sum.astype(jnp.bfloat16), 'tp')  216 us
    all_gather x1, waiting for transfers between devices, shards(): down_full = lax.all_gather(down_w, 'task', axis=1, tiled=True)  165 us
    dot_general x2, matrix products, apply(): lax.dot_general(features, second, (((0,), (0,)), ((), ())), preferred_ele...  29.5 us
    dot_general x2, matrix products, apply(): partial_sum = jnp.dot(active, down_full, preferred_element_type=jnp.float32)  29.1 us
    psum x2, blocking collectives, paired_sums(): return lax.psum((jnp.sum(vector * vector), jnp.sum(vector * image)), 'tp')  19.4 us
    reduce_sum x2, other arithmetic, apply(): jnp.sum(lax.all_gather(partial_sum.astype(jnp.bfloat16), 'tp'), axis=0)  16.3 us
  transfers between devices with their start and end apart: 3, of which 3 were waited for; matrix products, arithmetic and copies ran while one was open for 0% of the time, Pallas kernels for 0%

profile of v1, /device:TPU:0, one launch (start us, length us, event | category | flops | bytes accessed | tf_op | source)
XLA Modules:
  0.0 504.8 jit_solution(14668250362427639205)
XLA Ops:
  7.2 0.0 copy-start
  7.2 0.0 copy-start.1
  7.2 0.0 all-gather.6.cloned.1.call-start
  7.2 0.7 all-gather.6.cloned.1.call-update
  7.9 0.0 all-gather.8.cloned.1.call-start
  8.9 0.1 copy-done
  8.9 2.0 fusion.13
  10.9 165.4 %all-gather.6.cloned.1.call-done = bf16[2560,3584]{0,1:T(8,128)(2,1)} async-done(((bf16[2560,448]{0,1:T(8,128)(2,1)}), bf16[2560,3584]{0,1:T(8,128)(2,1)}) %all-gather.6.cloned.1.call-update) | async-done | bytes 18350096 | tf_op jit(solution)/shard_map/all_gather | solution.py:10
  176.4 0.0 copy-done.1
  176.4 14.4 %convolution_convert_fusion.1 = bf16[384,3584]{1,0:T(8,128)(2,1)} fusion(bf16[2560,3584]{0,1:T(8,128)(2,1)} %all-gather.6.cloned.1.call-done, bf16[384,64]{0,1:T(8,128)(2,1)S(1)} %fusion.13, f32[1,64,2560]{2,1,0:T(8,128)S(1)} %copy-done.1, bf16[1,384,2560]{2,1,0:T(8,128)(2,1)} %param.9, pred[384]{0:T(512)(128)(4,1)S(1)} %iota_compare_fusion), kind=kOutput, calls=%fused_computation.5 | convolution fusion | flops 7183466496 | bytes 23773568 | tf_op jit(solution)/shard_map/dot_general | solution.py:29
  190.8 0.0 all-gather.8.cloned.1.call-update
  190.8 0.0 all-gather.10.cloned.1.call-start
  191.5 106.9 %all-gather.8.cloned.1.call-done = bf16[1536,3584]{1,0:T(8,128)(2,1)} async-done(((bf16[384,3584]{1,0:T(8,128)(2,1)}), bf16[1536,3584]{1,0:T(8,128)(2,1)}) %all-gather.8.cloned.1.call-update) | async-done | bytes 11010064 | tf_op jit(solution)/shard_map/all_gather | solution.py:30
  298.5 8.2 %reduce_sum.61 = bf16[384,3584]{1,0:T(8,128)(2,1)} reduce(bf16[4,384,3584]{2,1,0:T(8,128)(2,1)} %bitcast.75, bf16[]{:T(256)} %constant.7.clone.1), dimensions={0}, to_apply=%region_2.3 | reduce | flops 4128768 | bytes 13762562 | tf_op jit(solution)/shard_map/reduce_sum | solution.py:30
  306.6 14.5 %fusion.17 = (f32[]{:T(128)}, f32[]{:T(128)}, f32[64,2560]{1,0:T(8,128)}) fusion(f32[1,64,2560]{2,1,0:T(8,128)S(1)} %copy-done.1, f32[]{:T(128)} %bitcast.73, f32[]{:T(128)S(6)} %convert_element_type.58, bf16[384,64]{0,1:T(8,128)(2,1)S(1)} %fusion.13, bf16[384,3584]{1,0:T(8,128)(2,1)} %reduce_sum.61, bf16[2560,3584]{0,1:T(8,128)(2,1)} %all-gather.6.cloned.1.call-done, ...), kind=kOutput, calls=%fused_computation.32 | convolution fusion | flops 7183237120 | bytes 24428944 | tf_op jit(solution)/shard_map/dot_general | solution.py:32
  321.1 9.8 %all-reduce.1 = (f32[]{:T(128)}, f32[]{:T(128)}) all-reduce(f32[]{:T(128)} %get-tuple-element.5, f32[]{:T(128)} %get-tuple-element.4), channel_id=1, replica_groups=mesh['task'=8,'tp'=4] {'tp'}, use_global_device_ids=true, to_apply=%region_1.2 | all-reduce | flops 2 | bytes 16 | tf_op jit(solution)/shard_map/psum | solution.py:38
  332.2 2.0 bitcast_subtract_fusion
  334.2 14.6 %convolution_convert_fusion = bf16[384,3584]{1,0:T(8,128)(2,1)} fusion(bf16[2560,3584]{0,1:T(8,128)(2,1)} %all-gather.6.cloned.1.call-done, bf16[384,64]{0,1:T(8,128)(2,1)S(1)} %fusion.13, f32[64,2560]{1,0:T(8,128)} %bitcast_subtract_fusion, bf16[1,384,2560]{2,1,0:T(8,128)(2,1)} %param.9, pred[384]{0:T(512)(128)(4,1)S(1)} %iota_compare_fusion), kind=kOutput, calls=%fused_computation.4 | convolution fusion | flops 7183630336 | bytes 23773568 | tf_op jit(solution)/shard_map/dot_general | solution.py:29
  348.8 0.0 all-gather.10.cloned.1.call-update
  348.9 109.4 %all-gather.10.cloned.1.call-done = bf16[1536,3584]{1,0:T(8,128)(2,1)} async-done(((bf16[384,3584]{1,0:T(8,128)(2,1)}), bf16[1536,3584]{1,0:T(8,128)(2,1)}) %all-gather.10.cloned.1.call-update) | async-done | bytes 11010064 | tf_op jit(solution)/shard_map/all_gather | solution.py:30
  458.3 8.2 %reduce_sum.64 = bf16[384,3584]{1,0:T(8,128)(2,1)} reduce(bf16[4,384,3584]{2,1,0:T(8,128)(2,1)} %bitcast.76, bf16[]{:T(256)} %constant.7.clone.1), dimensions={0}, to_apply=%region_7.8 | reduce | flops 4128768 | bytes 13762562 | tf_op jit(solution)/shard_map/reduce_sum | solution.py:30
  466.4 15.0 %multiply_reduce_fusion = (f32[]{:T(128)}, f32[]{:T(128)}, f32[64,2560]{1,0:T(8,128)}) fusion(f32[64,2560]{1,0:T(8,128)} %bitcast_subtract_fusion, f32[]{:T(128)} %bitcast.74, f32[]{:T(128)S(6)} %convert_element_type.58, bf16[384,64]{0,1:T(8,128)(2,1)S(1)} %fusion.13, bf16[384,3584]{1,0:T(8,128)(2,1)} %reduce_sum.64, ...), kind=kOutput, calls=%fused_computation.38 | convolution fusion | flops 7183237120 | bytes 24428944 | tf_op jit(solution)/shard_map/dot_general | solution.py:32
  481.4 9.6 %all-reduce = (f32[]{:T(128)}, f32[]{:T(128)}) all-reduce(f32[]{:T(128)} %get-tuple-element.3, f32[]{:T(128)} %get-tuple-element.2), channel_id=1, replica_groups=mesh['task'=8,'tp'=4] {'tp'}, use_global_device_ids=true, to_apply=%region_6.7 | all-reduce | flops 2 | bytes 16 | tf_op jit(solution)/shard_map/psum | solution.py:38
  495.5 2.7 subtract_bitcast_fusion
  (1 shorter events, 0.0 us)
Async XLA Ops:
  7.2 1.8 copy-start
  7.2 169.2 %copy-start.1 = (f32[1,64,2560]{2,1,0:T(8,128)S(1)}, f32[1,64,2560]{2,1,0:T(8,128)}, u32[]{:S(2)}) copy-start(f32[1,64,2560]{2,1,0:T(8,128)} %param.13) | copy-start | bytes 1966084
  7.2 169.2 %all-gather.6.cloned.1.call-start = ((), (), s32[]{:S(2)}) async-start(), calls=%async_computation | async-start | bytes 20643840 | tf_op jit(solution)/shard_map/all_gather | solution.py:10
  7.9 290.5 %all-gather.8.cloned.1.call-start = ((), (), s32[]{:S(2)}) async-start(), calls=%async_computation.1 | async-start | bytes 13762560 | tf_op jit(solution)/shard_map/all_gather | solution.py:30
  190.8 267.5 %all-gather.10.cloned.1.call-start = ((), (), s32[]{:S(2)}) async-start(), calls=%async_computation.2 | async-start | bytes 13762560 | tf_op jit(solution)/shard_map/all_gather | solution.py:30
Sparse Core Ops, SparseCore 0:
  9.6 166.6 all-gather.5
  190.9 107.4 all-gather.7
  349.0 109.2 all-gather.9
